TPU v7x, 32 devices: a whole 2x2x4 slice. The times are simulated.
32 devices in a mesh: ep: 16 (over z, y, x), tp: 2 (over core).
Axes of the slice: x: 2, y: 2, z: 4, core: 2. Of those that a mesh axis runs over, the one named last changes fastest.
Arguments:
- tokens: bfloat16 [2048, 2048], P('ep', 'tp'), may hold values from -6 to 6
- cotangent: bfloat16 [2048, 2048], P('ep', 'tp'), may hold values from -6 to 6
- expert_ids: int32 [2048, 6], P('ep'), may hold values from 0 to 15, all different within a row; in each aligned block of 128 rows (0 to 127, 128 to 255, ...) at most 64 rows name the same one
- gate_values: float32 [2048, 6], P('ep'), may hold values from 0.1 to 1
- w_gate: bfloat16 [16, 1408, 2048], P('ep', 'tp'), may hold values from -0.125 to 0.125
- w_up: bfloat16 [16, 1408, 2048], P('ep', 'tp'), may hold values from -0.125 to 0.125
- w_down: bfloat16 [16, 1408, 2048], P('ep', 'tp'), may hold values from -0.15625 to 0.15625
Outputs:
- input_grad: bfloat16 [2048, 2048], P('ep', 'tp')
- grad_gate: bfloat16 [16, 1408, 2048], P('ep', 'tp')
- grad_up: bfloat16 [16, 1408, 2048], P('ep', 'tp')
- grad_down: bfloat16 [16, 1408, 2048], P('ep', 'tp')
Inputs may be any that keep to these rules, and one draw needn't show every extreme that they name: `expert_ids`: each token names 6 different experts. Among the 128 tokens of one group, no expert is named more than 64 times.
All inputs are finite; a program needn't handle non-finite values.
Results may differ from a plain program's by a relative error of at most 0.017.
Values may be sent and summed in bfloat16 or wider, within the bound.
A program may use at most 64 MiB of HBM per device.

v0:
```python
import functools
import jax
import jax.numpy as jnp
from jax import lax
from jax.experimental import pallas as pl
from jax.experimental.pallas import tpu as pltpu
from jax.sharding import PartitionSpec as P


def outer_factor(count):
    outer = 1
    while outer * 2 * outer * 2 <= count and count % (outer * 2) == 0:
        outer *= 2
    return outer


def nt(left, right):
    return lax.dot_general(
        left, right, (((1,), (1,)), ((), ())), preferred_element_type=jnp.float32
    )


def tn(left, right):
    return lax.dot_general(
        left, right, (((0,), (0,)), ((), ())), preferred_element_type=jnp.float32
    )


def nn(left, right):
    return jnp.dot(left, right, preferred_element_type=jnp.float32)


def kernel(
    nz, npl, ntp, cap, mrows,
    tok, cot, meta, wg_hbm, wu_hbm, wd_hbm,
    ig, gg_hbm, gu_hbm, gd_hbm,
    zx, zc, zm, oh, grow, sx, sc, xe, ge, wg, wu, wd, at, bt, ht, dat, dbt,
    stage, red, redr, rows, rowr, part, partr,
    s_w, s_o, zs, zr, ps, pr, ls, ts, tr, ds, dr, rs, rr, rl, qs, qr,
):
    ep = lax.axis_index("ep")
    c = lax.axis_index("tp")
    z = ep // npl
    p = ep % npl
    width = tok.shape[1]
    batch = npl * cap
    steps = sorted(range(nz), key=lambda j: (min(j, nz - j), j))

    def zdev(j):
        return {"ep": ((z + j) % nz) * npl + p}

    def pdev(d):
        return {"ep": z * npl + (p + d) % npl}

    def tdev(d):
        return {"tp": (c + d) % ntp}

    def cols(core):
        return pl.ds(pl.multiple_of(core * width, width), width)

    def remote(src, dst, ssem, rsem, dev):
        return pltpu.make_async_remote_copy(
            src_ref=src, dst_ref=dst, send_sem=ssem, recv_sem=rsem,
            device_id=dev, device_id_type=pl.DeviceIdType.MESH,
        )

    weights = [
        pltpu.make_async_copy(h.at[0], v, s_w.at[i])
        for i, (h, v) in enumerate(((wg_hbm, wg), (wu_hbm, wu), (wd_hbm, wd)))
    ]
    for w in weights:
        w.start()

    barrier = pltpu.get_barrier_semaphore()
    peers = [zdev(j) for j in range(1, nz)]
    peers += [pdev(d) for d in range(1, npl)]
    peers += [tdev(d) for d in range(1, ntp)]
    for dev in peers:
        pl.semaphore_signal(barrier, inc=1, device_id=dev, device_id_type=pl.DeviceIdType.MESH)
    pl.semaphore_wait(barrier, len(peers))

    def zcopy(kind, j):
        src, dst = ((meta, zm), (tok, zx), (cot, zc))[kind]
        return remote(src, dst.at[j], zs.at[kind, j], zr.at[kind, j], zdev(j))

    for kind in (0, 1, 2):
        for j in steps[1:]:
            zcopy(kind, j).start()

    before = (
        lax.broadcasted_iota(jnp.int32, (128, 128), 0)
        < lax.broadcasted_iota(jnp.int32, (128, 128), 1)
    ).astype(jnp.bfloat16) if meta.shape[1] == 128 else None
    if before is None:
        n = meta.shape[1]
        before = (
            lax.broadcasted_iota(jnp.int32, (n, n), 0)
            < lax.broadcasted_iota(jnp.int32, (n, n), 1)
        ).astype(jnp.bfloat16)
    ntok = meta.shape[1]
    slot_iota = lax.broadcasted_iota(jnp.int32, (cap, ntok), 0).astype(jnp.float32)

    def build(j):
        m = meta[...] if j == 0 else zm[j]
        ids, gates = m[:mrows], m[mrows:]
        for d in range(npl):
            e = (z * npl + (p + d) % npl).astype(jnp.float32)
            hit = ids == e
            has = jnp.sum(jnp.where(hit, 1.0, 0.0), axis=0, keepdims=True)
            gate = jnp.sum(jnp.where(hit, gates, 0.0), axis=0, keepdims=True)
            pos = nn(jnp.broadcast_to(has, (16, ntok)).astype(jnp.bfloat16), before)[0:1]
            sel = jnp.where(slot_iota == pos, 1.0, 0.0) * has
            oh[j, d * cap:(d + 1) * cap, :] = sel.astype(jnp.bfloat16)
            grow[j, d * cap:(d + 1) * cap, :] = jnp.sum(sel * gate, axis=1, keepdims=True)

    def pcopy(kind, j, d):
        src, dst = ((sx, xe), (sc, ge))[kind]
        lines = pl.ds(j * batch + d * cap, cap)
        s, t = src.at[j, pl.ds(d * cap, cap), :], dst.at[lines, cols(c)]
        if d == 0:
            return pltpu.make_async_copy(s, t, ls.at[kind, j])
        return remote(s, t, ps.at[kind, j, d], pr.at[kind, j, d], pdev(d))

    def send_x(j):
        if j:
            zcopy(0, j).wait_recv()
            zcopy(1, j).wait_recv()
        build(j)
        block = tok[...] if j == 0 else zx[j]
        sx[j] = nn(oh[j], block).astype(jnp.bfloat16)
        for d in range(1, npl):
            pcopy(0, j, d).start()
        pcopy(0, j, 0).start()

    def send_c(j):
        if j:
            zcopy(2, j).wait_recv()
        block = cot[...] if j == 0 else zc[j]
        sc[j] = (nn(oh[j], block) * grow[j]).astype(jnp.bfloat16)
        for d in range(1, npl):
            pcopy(1, j, d).start()
        pcopy(1, j, 0).start()

    def tcopy(kind, j, d, owner):
        buf = (xe, ge)[kind]
        view = buf.at[pl.ds(j * batch, batch), cols(owner)]
        return remote(view, view, ts.at[kind, j, d], tr.at[kind, j, d], tdev(d))

    def forward(kind, j):
        for d in range(1, npl):
            pcopy(kind, j, d).wait_recv()
        pcopy(kind, j, 0).wait()
        for d in range(1, ntp):
            tcopy(kind, j, d, c).start()

    def arrive(kind, j):
        for d in range(1, ntp):
            tcopy(kind, j, d, (c + ntp - d) % ntp).wait_recv()

    def span(j):
        return pl.ds(j * batch, batch)

    def up(j):
        arrive(0, j)
        x = xe[j * batch:(j + 1) * batch, :]
        at[:, j * batch:(j + 1) * batch] = nt(wg[...], x)
        bt[:, j * batch:(j + 1) * batch] = nt(wu[...], x)

    def dcopy(j, d):
        return remote(
            red.at[j, :, cols((c + d) % ntp)], redr.at[j, d],
            ds.at[j, d], dr.at[j, d], tdev(d),
        )

    def down(j):
        arrive(1, j)
        lines = slice(j * batch, (j + 1) * batch)
        dh = nt(wd[...], ge[lines, :])
        a, b = at[:, lines], bt[:, lines]
        s = jax.nn.sigmoid(a)
        swish = a * s
        ht[:, lines] = (swish * b).astype(jnp.bfloat16)
        da = (dh * b * s * (1.0 + a * (1.0 - s))).astype(jnp.bfloat16)
        db = (dh * swish).astype(jnp.bfloat16)
        dat[:, lines] = da
        dbt[:, lines] = db
        red[j] = (tn(da, wg[...]) + tn(db, wu[...])).astype(jnp.bfloat16)
        for d in range(1, ntp):
            dcopy(j, d).start()

    def rcopy(j, d):
        lines = pl.ds(d * cap, cap)
        s, t = rows.at[j, lines, :], rowr.at[j, lines, :]
        if d == 0:
            return pltpu.make_async_copy(s, t, rl.at[j])
        return remote(s, t, rs.at[j, d], rr.at[j, d], pdev(npl - d))

    def back(j):
        total = red[j, :, cols(c)].astype(jnp.float32)
        for d in range(1, ntp):
            dcopy(j, d).wait_recv()
            total = total + redr[j, d].astype(jnp.float32)
        rows[j] = total.astype(jnp.bfloat16)
        for d in range(1, npl):
            rcopy(j, d).start()
        rcopy(j, 0).start()

    def qcopy(j):
        return remote(part.at[j], partr.at[j], qs.at[j], qr.at[j], zdev(nz - j))

    def combine(j):
        for d in range(1, npl):
            rcopy(j, d).wait_recv()
        rcopy(j, 0).wait()
        part[j] = tn(oh[j], rowr[j]).astype(jnp.bfloat16)
        if j:
            qcopy(j).start()

    tile = stage.shape[2]
    tiles = xe.shape[1] // tile

    def ocopy(hbm, slot, t):
        return pltpu.make_async_copy(
            stage.at[slot], hbm.at[0, :, pl.ds(pl.multiple_of(t * tile, tile), tile)], s_o.at[slot]
        )

    def grads(which):
        left, right, hbm = ((dat, xe, gg_hbm), (dbt, xe, gu_hbm), (ht, ge, gd_hbm))[which]

        @pl.loop(0, tiles)
        def _(t):
            slot = which * tiles + t
            here = pl.ds(pl.multiple_of(t * tile, tile), tile)
            stage[slot] = nn(left[...], right[:, here]).astype(jnp.bfloat16)
            ocopy(hbm, slot, t).start()

    def grads_done(which):
        hbm = (gg_hbm, gu_hbm, gd_hbm)[which]

        @pl.loop(0, tiles)
        def _(t):
            ocopy(hbm, which * tiles + t, t).wait()

    todo = []
    k = len(steps)
    send_x(steps[0])
    send_c(steps[0])
    for i in range(1, k):
        send_x(steps[i])
        forward(0, steps[i - 1])
        if i == 1:
            for w in weights:
                w.wait()
            forward(1, steps[0])
        if i >= 2:
            up(steps[i - 2])
    forward(0, steps[k - 1])
    if k >= 2:
        up(steps[k - 2])
    else:
        for w in weights:
            w.wait()
        forward(1, steps[0])
    down_order = list(steps)
    down(steps[0])
    for i in range(1, k):
        send_c(steps[i])
        if i == 1:
            up(steps[k - 1])
            back(steps[0])
        if i >= 2:
            forward(1, steps[i - 1])
            down(steps[i - 1])
            back(steps[i - 1])
            combine(steps[i - 2])
    if k == 1:
        up(steps[0])
    if k >= 2:
        forward(1, steps[k - 1])
        down(steps[k - 1])
        if k >= 3:
            combine(steps[k - 2])
        back(steps[k - 1])
        if k == 2:
            combine(steps[0])
    grads(0)
    combine(steps[k - 1])
    grads(1)
    grads(2)

    total = part[0].astype(jnp.float32)
    for j in range(1, nz):
        qcopy(j).wait_recv()
        total = total + partr[j].astype(jnp.float32)
    ig[...] = total.astype(jnp.bfloat16)
    for j in range(nz):
        if j:
            for kind in (0, 1, 2):
                zcopy(kind, j).wait_send()
            qcopy(j).wait_send()
        for d in range(1, npl):
            pcopy(0, j, d).wait_send()
            pcopy(1, j, d).wait_send()
            rcopy(j, d).wait_send()
        for d in range(1, ntp):
            tcopy(0, j, d, c).wait_send()
            tcopy(1, j, d, c).wait_send()
            dcopy(j, d).wait_send()
    for which in range(3):
        grads_done(which)


def local(nep, ntp, tokens, cotangent, expert_ids, gate_values, w_gate, w_up, w_down):
    tok_count, top = expert_ids.shape
    cap = max(2, tok_count * top * 4 // (nep * 3))
    nz = outer_factor(nep)
    npl = nep // nz
    width = tokens.shape[1]
    full = width * ntp
    hidden = w_gate.shape[1]
    batch = npl * cap
    count = nep * cap
    mrows = -(-top // 8) * 8
    pad = ((0, mrows - top), (0, 0))
    meta = jnp.concatenate(
        [
            jnp.pad(expert_ids.T.astype(jnp.float32), pad, constant_values=-1.0),
            jnp.pad(gate_values.T, pad),
        ],
        axis=0,
    )
    bf, f32 = jnp.bfloat16, jnp.float32
    vm = pltpu.VMEM
    dma = pltpu.SemaphoreType.DMA
    tile = min(512, full)
    scratch = [
        vm((nz, tok_count, width), bf), vm((nz, tok_count, width), bf),
        vm((nz, 2 * mrows, tok_count), f32),
        vm((nz, batch, tok_count), bf), vm((nz, batch, 1), f32),
        vm((nz, batch, width), bf), vm((nz, batch, width), bf),
        vm((count, full), bf), vm((count, full), bf),
        vm((hidden, full), bf), vm((hidden, full), bf), vm((hidden, full), bf),
        vm((hidden, count), f32), vm((hidden, count), f32),
        vm((hidden, count), bf), vm((hidden, count), bf), vm((hidden, count), bf),
        vm((3 * (full // tile), hidden, tile), bf),
        vm((nz, batch, full), bf), vm((nz, ntp, batch, width), bf),
        vm((nz, batch, width), bf), vm((nz, batch, width), bf),
        vm((nz, tok_count, width), bf), vm((nz, tok_count, width), bf),
        dma((3,)), dma((3 * (full // tile),)),
        dma((3, nz)), dma((3, nz)),
        dma((2, nz, npl)), dma((2, nz, npl)), dma((2, nz)),
        dma((2, nz, ntp)), dma((2, nz, ntp)),
        dma((nz, ntp)), dma((nz, ntp)),
        dma((nz, npl)), dma((nz, npl)), dma((nz,)),
        dma((nz,)), dma((nz,)),
    ]
    inside = pl.BlockSpec(memory_space=pltpu.VMEM)
    outside = pl.BlockSpec(memory_space=pl.ANY)
    shape = jax.ShapeDtypeStruct
    return pl.pallas_call(
        functools.partial(kernel, nz, npl, ntp, cap, mrows),
        out_shape=(
            shape(tokens.shape, bf), shape(w_gate.shape, bf),
            shape(w_up.shape, bf), shape(w_down.shape, bf),
        ),
        in_specs=[inside] * 3 + [outside] * 3,
        out_specs=(inside, outside, outside, outside),
        scratch_shapes=scratch,
        compiler_params=pltpu.CompilerParams(
            collective_id=0, has_side_effects=True, vmem_limit_bytes=67043328
        ),
    )(tokens, cotangent, meta, w_gate, w_up, w_down)


def solution(mesh):
    in_specs = (
        P("ep", "tp"), P("ep", "tp"), P("ep", None), P("ep", None),
        P("ep", "tp", None), P("ep", "tp", None), P("ep", "tp", None),
    )
    out_specs = (P("ep", "tp"), P("ep", "tp", None), P("ep", "tp", None), P("ep", "tp", None))
    body = functools.partial(local, mesh.shape["ep"], mesh.shape["tp"])
    return jax.shard_map(body, mesh=mesh, in_specs=in_specs, out_specs=out_specs, check_vma=False)
```

profile of v0, /device:TPU:0, one launch (start us, length us, event | category | flops | bytes accessed | tf_op | source)
XLA Modules:
  0.0 125.7 jit_solution(4334618664663804805)
XLA Ops:
  0.6 0.7 convert_bitcast_fusion
  1.3 1.3 %select_maximum_fusion.meta = f32[16,128]{1,0:T(8,128)} fusion(f32[6,128]{1,0:T(8,128)} %bitcast.3, f32[6,128]{1,0:T(8,128)S(1)} %convert_bitcast_fusion), kind=kLoop, calls=%fused_computation | loop fusion | flops 10240 | bytes 14336 | tf_op jit(solution)/shard_map/concatenate | solution.py:325
  2.6 113.1 %shard_map.102 = (bf16[128,1024]{1,0:T(8,128)(2,1)}, bf16[1,704,2048]{2,1,0:T(8,128)(2,1)}, bf16[1,704,2048]{2,1,0:T(8,128)(2,1)}, bf16[1,704,2048]{2,1,0:T(8,128)(2,1)}) custom-call(bf16[128,1024]{1,0:T(8,128)(2,1)} %tok.1, bf16[128,1024]{1,0:T(8,128)(2,1)} %cot.1, f32[16,128]{1,0:T(8,128)} %select_maximum_fusion.meta, bf16[1,704,2048]{2,1,0:T(8,128)(2,1)} %wg_hbm.1, ...), custom_call_target="tpu_custom_call" | custom-call | tf_op jit(solution)/shard_map/pallas_call | solution.py:360
  115.7 1.7 %copy.15 = bf16[128,1024]{1,0:T(8,128)(2,1)} copy(bf16[128,1024]{1,0:T(8,128)(2,1)} %get-tuple-element.8) | data formatting | bytes 524288
  117.4 0.0 copy-start.1
  117.4 3.9 %copy.16 = bf16[1,704,2048]{2,1,0:T(8,128)(2,1)} copy(bf16[1,704,2048]{2,1,0:T(8,128)(2,1)} %get-tuple-element.9) | data formatting | bytes 5767168
  121.3 0.0 copy-done.1
  121.3 0.0 copy-start
  121.3 1.6 %copy.17 = bf16[1,704,2048]{2,1,0:T(8,128)(2,1)} copy(bf16[1,704,2048]{2,1,0:T(8,128)(2,1)S(1)} %copy-done.1) | data formatting | bytes 5767168
  122.9 1.3 %copy-done = bf16[1,704,2048]{2,1,0:T(8,128)(2,1)S(1)} copy-done((bf16[1,704,2048]{2,1,0:T(8,128)(2,1)S(1)}, bf16[1,704,2048]{2,1,0:T(8,128)(2,1)}, u32[]{:S(2)}) %copy-start) | copy-done | bytes 2883608
  124.1 1.6 %copy.18 = bf16[1,704,2048]{2,1,0:T(8,128)(2,1)} copy(bf16[1,704,2048]{2,1,0:T(8,128)(2,1)S(1)} %copy-done) | data formatting | bytes 5767168
Async XLA Ops:
  117.4 3.9 %copy-start.1 = (bf16[1,704,2048]{2,1,0:T(8,128)(2,1)S(1)}, bf16[1,704,2048]{2,1,0:T(8,128)(2,1)}, u32[]{:S(2)}) copy-start(bf16[1,704,2048]{2,1,0:T(8,128)(2,1)} %get-tuple-element.10) | copy-start | bytes 8650756
  121.3 2.9 %copy-start = (bf16[1,704,2048]{2,1,0:T(8,128)(2,1)S(1)}, bf16[1,704,2048]{2,1,0:T(8,128)(2,1)}, u32[]{:S(2)}) copy-start(bf16[1,704,2048]{2,1,0:T(8,128)(2,1)} %get-tuple-element.11) | copy-start | bytes 8650756
where the time goes:
time: 126 us
  Pallas kernels  113 us (90%)
  local copies, waits for them, and re-layouts  10 us (8%)
  other arithmetic  1.98 us (2%)
    pallas_call x1, Pallas kernels, local(): pl.pallas_call(functools.partial(kernel, nz, npl, ntp, cap, mrows), out_s...  113 us
    unnamed x8, local copies, waits for them, and re-layouts  10 us

commit v1 on v0

v1 whole, which is shorter than its diff:
```python
import functools
import jax
import jax.numpy as jnp
from jax import lax
from jax.experimental import pallas as pl
from jax.experimental.pallas import tpu as pltpu
from jax.sharding import PartitionSpec as P


def outer_factor(count):
    outer = 1
    while outer * 2 * outer * 2 <= count and count % (outer * 2) == 0:
        outer *= 2
    return outer


def nt(left, right):
    return lax.dot_general(
        left, right, (((1,), (1,)), ((), ())), preferred_element_type=jnp.float32
    )


def tn(left, right):
    return lax.dot_general(
        left, right, (((0,), (0,)), ((), ())), preferred_element_type=jnp.float32
    )


def nn(left, right):
    return jnp.dot(left, right, preferred_element_type=jnp.float32)


def kernel(
    nz, npl, ntp, cap,
    tok_hbm, cot_hbm, ids_hbm, gat_hbm, wg_hbm, wu_hbm, wd_hbm,
    ig, gg, gu, gd,
    tok, cot, ids, gat, zx, zc, zi, zg,
    oh, grow, sx, sc, xe, ge, wg, wu, wd, at, bt, ht, dat, dbt,
    red, redr, rows, rowr, part, partr,
    s_i, s_w, zs, zr, ps, pr, ls, ts, tr, ds, dr, rs, rr, rl, qs, qr,
):
    ep = lax.axis_index("ep")
    c = lax.axis_index("tp")
    z = ep // npl
    p = ep % npl
    width = tok.shape[1]
    batch = npl * cap
    half = max(1, nz // 2)
    upper = z // half if nz > 1 else 0
    w = z + upper * (nz - 1 - 2 * z)
    inner = w > 0

    def mirror(v):
        return v + upper * (nz - 1 - 2 * v)

    def source(i):
        over = (w + i) // nz
        return mirror((1 - over) * (w + i) + over * (nz - 1 - i))

    def zdev(j):
        return {"ep": ((z + j) % nz) * npl + p}

    def pdev(d):
        return {"ep": z * npl + (p + d) % npl}

    def tdev(d):
        return {"tp": (c + d) % ntp}

    def cols(core):
        return pl.ds(pl.multiple_of(core * width, width), width)

    def remote(src, dst, ssem, rsem, dev):
        return pltpu.make_async_remote_copy(
            src_ref=src, dst_ref=dst, send_sem=ssem, recv_sem=rsem,
            device_id=dev, device_id_type=pl.DeviceIdType.MESH,
        )

    inputs = [
        pltpu.make_async_copy(h, v, s_i.at[i])
        for i, (h, v) in enumerate(
            ((ids_hbm, ids), (gat_hbm, gat), (tok_hbm, tok), (cot_hbm, cot))
        )
    ]
    for copy in inputs:
        copy.start()

    barrier = pltpu.get_barrier_semaphore()
    peers = [{"ep": mirror(w + 1) * npl + p}] if nz > 1 else []
    peers += [pdev(d) for d in range(1, npl)]
    peers += [tdev(d) for d in range(1, ntp)]

    def greet(dev):
        pl.semaphore_signal(barrier, inc=1, device_id=dev, device_id_type=pl.DeviceIdType.MESH)

    for dev in peers:
        greet(dev)
    if nz > 1:

        @pl.when(inner)
        def _():
            greet({"ep": mirror(w - 1) * npl + p})

    pl.semaphore_wait(barrier, len(peers) + (w + nz - 1) // nz)

    zown = (ids, gat, tok, cot)
    zin = (zi, zg, zx, zc)

    def zsend(kind, block, to):
        slot = mirror(block)
        return remote(
            zin[kind].at[slot], zin[kind].at[slot], zs.at[kind, slot], zr.at[kind, slot],
            {"ep": mirror(to) * npl + p},
        )

    def zfirst(kind, side):
        sem = zs.at[kind, z if side > 0 else nz]
        return remote(
            zown[kind], zin[kind].at[z], sem, zr.at[kind, z], {"ep": mirror(w + side) * npl + p}
        )

    def relays(k):
        found = []
        if k < nz:
            found.append((inner if k <= nz - half else inner & (w + k < nz), k, -1))
        if k < half:
            found.append((w >= k, -k, 1))
        return found

    for kind in range(4):
        inputs[kind].wait()
        if nz > 1:
            zfirst(kind, 1).start()

            @pl.when(inner)
            def _():
                zfirst(kind, -1).start()

    weights = [
        pltpu.make_async_copy(h.at[0], v, s_w.at[i])
        for i, (h, v) in enumerate(((wg_hbm, wg), (wu_hbm, wu), (wd_hbm, wd)))
    ]
    for copy in weights:
        copy.start()

    def kinds(kind):
        return (0, 1, 2) if kind == 0 else (3,)

    def early(kind, k):
        for holds, off, side in relays(k):

            @pl.when(holds)
            def _():
                for part_ in kinds(kind):
                    copy = zsend(part_, w + off, w + side)
                    copy.wait_recv()
                    copy.start()

    def late(kind, i):
        @pl.when(w == 0)
        def _():
            for part_ in kinds(kind):
                zsend(part_, i, w).wait_recv()

    ntok = ids.shape[1]
    before = (
        lax.broadcasted_iota(jnp.int32, (ntok, ntok), 0)
        < lax.broadcasted_iota(jnp.int32, (ntok, ntok), 1)
    ).astype(jnp.bfloat16)
    slot_iota = lax.broadcasted_iota(jnp.int32, (cap, ntok), 0).astype(jnp.float32)

    def build(j):
        named = ids[...] if j == 0 else zi[source(j)]
        gates = gat[...] if j == 0 else zg[source(j)]
        for d in range(npl):
            hit = named == z * npl + (p + d) % npl
            has = jnp.sum(jnp.where(hit, 1.0, 0.0), axis=0, keepdims=True)
            gate = jnp.sum(jnp.where(hit, gates, 0.0), axis=0, keepdims=True)
            pos = nn(jnp.broadcast_to(has, (16, ntok)).astype(jnp.bfloat16), before)[0:1]
            sel = jnp.where(slot_iota == pos, 1.0, 0.0) * has
            oh[j, d * cap:(d + 1) * cap, :] = sel.astype(jnp.bfloat16)
            grow[j, d * cap:(d + 1) * cap, :] = jnp.sum(sel * gate, axis=1, keepdims=True)

    def pcopy(kind, j, d):
        src, dst = ((sx, xe), (sc, ge))[kind]
        lines = pl.ds(j * batch + d * cap, cap)
        s, t = src.at[j, pl.ds(d * cap, cap), :], dst.at[lines, cols(c)]
        if d == 0:
            return pltpu.make_async_copy(s, t, ls.at[kind, j])
        return remote(s, t, ps.at[kind, j, d], pr.at[kind, j, d], pdev(d))

    def send_x(j):
        if j:
            late(0, j)
        build(j)
        block = tok[...] if j == 0 else zx[source(j)]
        sx[j] = nn(oh[j], block).astype(jnp.bfloat16)
        for d in range(1, npl):
            pcopy(0, j, d).start()
        pcopy(0, j, 0).start()

    def send_c(j):
        if j:
            late(1, j)
        block = cot[...] if j == 0 else zc[source(j)]
        sc[j] = (nn(oh[j], block) * grow[j]).astype(jnp.bfloat16)
        for d in range(1, npl):
            pcopy(1, j, d).start()
        pcopy(1, j, 0).start()

    def tcopy(kind, j, d, q, owner):
        buf = (xe, ge)[kind]
        view = buf.at[pl.ds(j * batch + q * cap, cap), cols(owner)]
        return remote(view, view, ts.at[kind, j, q, d], tr.at[kind, j, q, d], tdev(d))

    def forward(kind, j):
        for q in range(npl):
            if q:
                pcopy(kind, j, q).wait_recv()
            else:
                pcopy(kind, j, 0).wait()
            for d in range(1, ntp):
                tcopy(kind, j, d, q, c).start()

    def arrive(kind, j):
        for q in range(npl):
            for d in range(1, ntp):
                tcopy(kind, j, d, q, (c + ntp - d) % ntp).wait_recv()

    def up(j):
        arrive(0, j)
        x = xe[j * batch:(j + 1) * batch, :]
        at[:, j * batch:(j + 1) * batch] = nt(wg[...], x)
        bt[:, j * batch:(j + 1) * batch] = nt(wu[...], x)

    def dcopy(j, d):
        return remote(
            red.at[j, :, cols((c + d) % ntp)], redr.at[j, d],
            ds.at[j, d], dr.at[j, d], tdev(d),
        )

    def down(j):
        arrive(1, j)
        lines = slice(j * batch, (j + 1) * batch)
        dh = nt(wd[...], ge[lines, :])
        a, b = at[:, lines], bt[:, lines]
        s = jax.nn.sigmoid(a)
        swish = a * s
        ht[:, lines] = (swish * b).astype(jnp.bfloat16)
        da = (dh * b * s * (1.0 + a * (1.0 - s))).astype(jnp.bfloat16)
        db = (dh * swish).astype(jnp.bfloat16)
        dat[:, lines] = da
        dbt[:, lines] = db
        for d in [*range(1, ntp), 0]:
            here = cols((c + d) % ntp)
            red[j, :, here] = (tn(da, wg[:, here]) + tn(db, wu[:, here])).astype(jnp.bfloat16)
            if d:
                dcopy(j, d).start()

    def rcopy(j, d):
        lines = pl.ds(d * cap, cap)
        s, t = rows.at[j, lines, :], rowr.at[j, lines, :]
        if d == 0:
            return pltpu.make_async_copy(s, t, rl.at[j])
        return remote(s, t, rs.at[j, d], rr.at[j, d], pdev(npl - d))

    def back(j):
        total = red[j, :, cols(c)].astype(jnp.float32)
        for d in range(1, ntp):
            dcopy(j, d).wait_recv()
            total = total + redr[j, d].astype(jnp.float32)
        rows[j] = total.astype(jnp.bfloat16)
        for d in range(1, npl):
            rcopy(j, d).start()
        rcopy(j, 0).start()

    def qcopy(j):
        return remote(
            part.at[j], partr.at[z], qs.at[j], qr.at[z], {"ep": source(j) * npl + p}
        )

    def qwait(j):
        here = source(j)
        remote(part.at[j], partr.at[here], qs.at[j], qr.at[here], zdev(1)).wait_recv()

    def combine(j):
        for d in range(1, npl):
            rcopy(j, d).wait_recv()
        rcopy(j, 0).wait()
        part[j] = tn(oh[j], rowr[j]).astype(jnp.bfloat16)
        if j:
            qcopy(j).start()

    tile = min(512, xe.shape[1])

    def grads(which):
        left, right, out = ((dat, xe, gg), (dbt, xe, gu), (ht, ge, gd))[which]

        @pl.loop(0, xe.shape[1] // tile)
        def _(t):
            here = pl.ds(pl.multiple_of(t * tile, tile), tile)
            out[0, :, here] = nn(left[...], right[:, here]).astype(jnp.bfloat16)

    last = nz - 1
    send_x(0)
    send_c(0)
    forward(0, 0)
    for i in range(1, nz):
        early(0, i)
        send_x(i)
        if i == 1:
            weights[0].wait()
            weights[1].wait()
        up(i - 1)
        forward(1, i - 1)
        early(1, i)
        send_c(i)
        if i == 1:
            weights[2].wait()
        if i == last:
            for j in range(1, last - 1):
                back(j)
        down(i - 1)
        forward(0, i)
    if nz == 1:
        for copy in weights:
            copy.wait()
    if last > 1:
        back(last - 1)
    up(last)
    forward(1, last)
    down(last)
    if last:
        back(last)
    for j in range(1, last - 1):
        combine(j)
    grads(0)
    if last > 1:
        combine(last - 1)
    back(0)
    grads(1)
    if last:
        combine(last)
    grads(2)
    combine(0)

    total = part[0].astype(jnp.float32)
    for j in range(1, nz):
        qwait(j)
        total = total + partr[source(j)].astype(jnp.float32)
    ig[...] = total.astype(jnp.bfloat16)
    if nz > 1:
        for kind in range(4):
            zfirst(kind, 1).wait_send()

            @pl.when(inner)
            def _():
                zfirst(kind, -1).wait_send()

        for k in range(1, nz):
            for holds, off, side in relays(k):

                @pl.when(holds)
                def _():
                    for kind in range(4):
                        zsend(kind, w + off, w + side).wait_send()

    for j in range(nz):
        if j:
            qcopy(j).wait_send()
        for d in range(1, npl):
            pcopy(0, j, d).wait_send()
            pcopy(1, j, d).wait_send()
            rcopy(j, d).wait_send()
        for d in range(1, ntp):
            for q in range(npl):
                tcopy(0, j, d, q, c).wait_send()
                tcopy(1, j, d, q, c).wait_send()
            dcopy(j, d).wait_send()


def finish(ig, gg, gu, gd, ig_hbm, gg_hbm, gu_hbm, gd_hbm, sem):
    copies = [
        pltpu.make_async_copy(v, h, sem.at[i])
        for i, (v, h) in enumerate(
            ((gg, gg_hbm), (gu, gu_hbm), (gd, gd_hbm), (ig, ig_hbm))
        )
    ]
    for copy in copies:
        copy.start()
    for copy in copies:
        copy.wait()


def local(nep, ntp, tokens, cotangent, expert_ids, gate_values, w_gate, w_up, w_down):
    tok_count, top = expert_ids.shape
    cap = max(2, tok_count * top * 4 // (nep * 3))
    nz = outer_factor(nep)
    npl = nep // nz
    width = tokens.shape[1]
    full = width * ntp
    hidden = w_gate.shape[1]
    batch = npl * cap
    count = nep * cap
    bf, f32 = jnp.bfloat16, jnp.float32
    vm = pltpu.VMEM
    dma = pltpu.SemaphoreType.DMA
    scratch = [
        vm((tok_count, width), bf), vm((tok_count, width), bf),
        vm((top, tok_count), jnp.int32), vm((top, tok_count), f32),
        vm((nz, tok_count, width), bf), vm((nz, tok_count, width), bf),
        vm((nz, top, tok_count), jnp.int32), vm((nz, top, tok_count), f32),
        vm((nz, batch, tok_count), bf), vm((nz, batch, 1), f32),
        vm((nz, batch, width), bf), vm((nz, batch, width), bf),
        vm((count, full), bf), vm((count, full), bf),
        vm((hidden, full), bf), vm((hidden, full), bf), vm((hidden, full), bf),
        vm((hidden, count), f32), vm((hidden, count), f32),
        vm((hidden, count), bf), vm((hidden, count), bf), vm((hidden, count), bf),
        vm((nz, batch, full), bf), vm((nz, ntp, batch, width), bf),
        vm((nz, batch, width), bf), vm((nz, batch, width), bf),
        vm((nz, tok_count, width), bf), vm((nz, tok_count, width), bf),
        dma((4,)), dma((3,)),
        dma((4, nz + 1)), dma((4, nz)),
        dma((2, nz, npl)), dma((2, nz, npl)), dma((2, nz)),
        dma((2, nz, npl, ntp)), dma((2, nz, npl, ntp)),
        dma((nz, ntp)), dma((nz, ntp)),
        dma((nz, npl)), dma((nz, npl)), dma((nz,)),
        dma((nz,)), dma((nz,)),
    ]
    inside = pl.BlockSpec(memory_space=pltpu.VMEM)
    outside = pl.BlockSpec(memory_space=pl.ANY)
    shapes = [tokens.shape, w_gate.shape, w_up.shape, w_down.shape]
    held = pl.pallas_call(
        functools.partial(kernel, nz, npl, ntp, cap),
        out_shape=tuple(vm(shape, bf) for shape in shapes),
        in_specs=[outside] * 7,
        out_specs=(inside,) * 4,
        scratch_shapes=scratch,
        compiler_params=pltpu.CompilerParams(
            collective_id=0, has_side_effects=True, vmem_limit_bytes=50 * 1024 * 1024
        ),
    )(tokens, cotangent, expert_ids.T, gate_values.T, w_gate, w_up, w_down)
    return pl.pallas_call(
        finish,
        out_shape=tuple(jax.ShapeDtypeStruct(shape, bf) for shape in shapes),
        in_specs=[inside] * 4,
        out_specs=(outside,) * 4,
        scratch_shapes=[dma((4,))],
        compiler_params=pltpu.CompilerParams(vmem_limit_bytes=1024 * 1024),
    )(*(pltpu.with_memory_space_constraint(value, pltpu.MemorySpace.VMEM) for value in held))


def solution(mesh):
    in_specs = (
        P("ep", "tp"), P("ep", "tp"), P("ep", None), P("ep", None),
        P("ep", "tp", None), P("ep", "tp", None), P("ep", "tp", None),
    )
    out_specs = (P("ep", "tp"), P("ep", "tp", None), P("ep", "tp", None), P("ep", "tp", None))
    body = functools.partial(local, mesh.shape["ep"], mesh.shape["tp"])
    return jax.shard_map(body, mesh=mesh, in_specs=in_specs, out_specs=out_specs, check_vma=False)
```

time: 126 us -> 93.3 us (0.74)
  Pallas kernels: 113 us -> 92.3 us
  local copies, waits for them, and re-layouts: 10 us -> 0 us
  other arithmetic: 1.98 us -> 0 us
    pallas_call x1 -> x2, Pallas kernels: 113 us -> 92.3 us  [the longest x1 88.8 us: local(): pl.pallas_call(functools.partial(kernel, nz, npl, ntp, cap), out_shape=tu...]
    unnamed x8 -> x0, local copies, waits for them, and re-layouts: 10 us -> none
    concatenate x1 -> x0, other arithmetic: 1.29 us -> none  [local(): jnp.concatenate([jnp.pad(expert_ids.T.astype(jnp.float32), pad, constant_...]
where the time goes in v1:
time: 93.3 us; the launch traced here: 93.1 us
  Pallas kernels  92.3 us (99%)
    pallas_call x1, Pallas kernels, local(): pl.pallas_call(functools.partial(kernel, nz, npl, ntp, cap), out_shape=tu...  88.8 us
    pallas_call x1, Pallas kernels, local(): pl.pallas_call(finish, out_shape=tuple((jax.ShapeDtypeStruct(shape, bf) f...  3.52 us

profile of v1, /device:TPU:0, one launch (start us, length us, event | category | flops | bytes accessed | tf_op | source)
XLA Modules:
  0.0 93.1 jit_solution(12437007284750424783)
XLA Ops:
  0.6 88.8 %shard_map.102 = (bf16[128,1024]{1,0:T(8,128)(2,1)S(1)}, bf16[1,704,2048]{2,1,0:T(8,128)(2,1)S(1)}, bf16[1,704,2048]{2,1,0:T(8,128)(2,1)S(1)}, bf16[1,704,2048]{2,1,0:T(8,128)(2,1)S(1)}) custom-call(bf16[128,1024]{1,0:T(8,128)(2,1)} %tok_hbm.1, bf16[128,1024]{1,0:T(8,128)(2,1)} %cot_hbm.1, s32[6,128]{1,0:T(8,128)} %bitcast.2, f32[6,128]{1,0:T(8,128)} %bitcast.3, ...), custom_call_target="tpu_custom_call" | custom-call | tf_op jit(solution)/shard_map/pallas_call | solution.py:432
  89.5 3.5 %shard_map.103 = (bf16[128,1024]{1,0:T(8,128)(2,1)}, bf16[1,704,2048]{2,1,0:T(8,128)(2,1)}, bf16[1,704,2048]{2,1,0:T(8,128)(2,1)}, bf16[1,704,2048]{2,1,0:T(8,128)(2,1)}) custom-call(bf16[128,1024]{1,0:T(8,128)(2,1)S(1)} %get-tuple-element.8.ig, bf16[1,704,2048]{2,1,0:T(8,128)(2,1)S(1)} %get-tuple-element.9.gg, ...), custom_call_target="tpu_custom_call" | custom-call | tf_op jit(solution)/shard_map/pallas_call | solution.py:442

commit v2 on v1

--- a/solution.py
+++ b/solution.py
@@ -36,8 +36,8 @@
     ig, gg, gu, gd,
     tok, cot, ids, gat, zx, zc, zi, zg,
     oh, grow, sx, sc, xe, ge, wg, wu, wd, at, bt, ht, dat, dbt,
-    red, redr, rows, rowr, part, partr,
-    s_i, s_w, zs, zr, ps, pr, ls, ts, tr, ds, dr, rs, rr, rl, qs, qr,
+    red, redr, rows, rowr, part, partr, near, seen, home, homer, acc,
+    s_i, s_w, zs, zr, ps, pr, ls, ts, tr, ds, dr, rs, rr, rl, qs, qr, ns, nr, es, er, hs, hr,
 ):
     ep = lax.axis_index("ep")
     c = lax.axis_index("tp")
@@ -54,8 +54,9 @@
         return v + upper * (nz - 1 - 2 * v)
 
     def source(i):
-        over = (w + i) // nz
-        return mirror((1 - over) * (w + i) + over * (nz - 1 - i))
+        d = (i + 1) // 2
+        near_ = (w - d + nz) // nz
+        return mirror(near_ * (w + (d if i % 2 else -d)) + (1 - near_) * i)
 
     def zdev(j):
         return {"ep": ((z + j) % nz) * npl + p}
@@ -99,8 +100,6 @@
         @pl.when(inner)
         def _():
             greet({"ep": mirror(w - 1) * npl + p})
-
-    pl.semaphore_wait(barrier, len(peers) + (w + nz - 1) // nz)
 
     zown = (ids, gat, tok, cot)
     zin = (zi, zg, zx, zc)
@@ -126,22 +125,6 @@
             found.append((w >= k, -k, 1))
         return found
 
-    for kind in range(4):
-        inputs[kind].wait()
-        if nz > 1:
-            zfirst(kind, 1).start()
-
-            @pl.when(inner)
-            def _():
-                zfirst(kind, -1).start()
-
-    weights = [
-        pltpu.make_async_copy(h.at[0], v, s_w.at[i])
-        for i, (h, v) in enumerate(((wg_hbm, wg), (wu_hbm, wu), (wd_hbm, wd)))
-    ]
-    for copy in weights:
-        copy.start()
-
     def kinds(kind):
         return (0, 1, 2) if kind == 0 else (3,)
 
@@ -168,15 +151,22 @@
     ).astype(jnp.bfloat16)
     slot_iota = lax.broadcasted_iota(jnp.int32, (cap, ntok), 0).astype(jnp.float32)
 
+    def pall(kind, j):
+        view = (sx, sc)[kind].at[j, pl.ds(cap, batch - cap), :]
+        return remote(view, view, ps.at[kind, j], pr.at[kind, j, 0], pdev(1 % npl))
+
+    def choose(named, e):
+        hit = named == e
+        has = jnp.sum(jnp.where(hit, 1.0, 0.0), axis=0, keepdims=True)
+        pos = nn(jnp.broadcast_to(has, (16, ntok)).astype(jnp.bfloat16), before)[0:1]
+        return hit, jnp.where(slot_iota == pos, 1.0, 0.0) * has
+
     def build(j):
         named = ids[...] if j == 0 else zi[source(j)]
         gates = gat[...] if j == 0 else zg[source(j)]
         for d in range(npl):
-            hit = named == z * npl + (p + d) % npl
-            has = jnp.sum(jnp.where(hit, 1.0, 0.0), axis=0, keepdims=True)
+            hit, sel = choose(named, z * npl + (p + d) % npl)
             gate = jnp.sum(jnp.where(hit, gates, 0.0), axis=0, keepdims=True)
-            pos = nn(jnp.broadcast_to(has, (16, ntok)).astype(jnp.bfloat16), before)[0:1]
-            sel = jnp.where(slot_iota == pos, 1.0, 0.0) * has
             oh[j, d * cap:(d + 1) * cap, :] = sel.astype(jnp.bfloat16)
             grow[j, d * cap:(d + 1) * cap, :] = jnp.sum(sel * gate, axis=1, keepdims=True)
 
@@ -186,31 +176,36 @@
         s, t = src.at[j, pl.ds(d * cap, cap), :], dst.at[lines, cols(c)]
         if d == 0:
             return pltpu.make_async_copy(s, t, ls.at[kind, j])
-        return remote(s, t, ps.at[kind, j, d], pr.at[kind, j, d], pdev(d))
-
-    def send_x(j):
-        if j:
-            late(0, j)
+        return remote(s, t, ps.at[kind, j], pr.at[kind, j, d - 1], pdev(d))
+
+    def pick_x(j):
         build(j)
         block = tok[...] if j == 0 else zx[source(j)]
         sx[j] = nn(oh[j], block).astype(jnp.bfloat16)
-        for d in range(1, npl):
-            pcopy(0, j, d).start()
-        pcopy(0, j, 0).start()
-
-    def send_c(j):
-        if j:
-            late(1, j)
+
+    def pick_c(j):
         block = cot[...] if j == 0 else zc[source(j)]
         sc[j] = (nn(oh[j], block) * grow[j]).astype(jnp.bfloat16)
+
+    def spread(kind, j):
         for d in range(1, npl):
-            pcopy(1, j, d).start()
-        pcopy(1, j, 0).start()
-
-    def tcopy(kind, j, d, q, owner):
+            pcopy(kind, j, d).start()
+        pcopy(kind, j, 0).start()
+
+    def send_x(j):
+        late(0, j)
+        pick_x(j)
+        spread(0, j)
+
+    def send_c(j):
+        late(1, j)
+        pick_c(j)
+        spread(1, j)
+
+    def tcopy(kind, j, d, q, count, owner):
         buf = (xe, ge)[kind]
-        view = buf.at[pl.ds(j * batch + q * cap, cap), cols(owner)]
-        return remote(view, view, ts.at[kind, j, q, d], tr.at[kind, j, q, d], tdev(d))
+        view = buf.at[pl.ds(j * batch + q * cap, count * cap), cols(owner)]
+        return remote(view, view, ts.at[kind, j, d - 1], tr.at[kind, j, d - 1], tdev(d))
 
     def forward(kind, j):
         for q in range(npl):
@@ -219,12 +214,11 @@
             else:
                 pcopy(kind, j, 0).wait()
             for d in range(1, ntp):
-                tcopy(kind, j, d, q, c).start()
+                tcopy(kind, j, d, q, 1, c).start()
 
     def arrive(kind, j):
-        for q in range(npl):
-            for d in range(1, ntp):
-                tcopy(kind, j, d, q, (c + ntp - d) % ntp).wait_recv()
+        for d in range(1, ntp):
+            tcopy(kind, j, d, 0, npl, (c + ntp - d) % ntp).wait_recv()
 
     def up(j):
         arrive(0, j)
@@ -234,8 +228,8 @@
 
     def dcopy(j, d):
         return remote(
-            red.at[j, :, cols((c + d) % ntp)], redr.at[j, d],
-            ds.at[j, d], dr.at[j, d], tdev(d),
+            red.at[j, :, cols((c + d) % ntp)], redr.at[j, d - 1],
+            ds.at[j, d - 1], dr.at[j, d - 1], tdev(d),
         )
 
     def down(j):
@@ -261,18 +255,82 @@
         s, t = rows.at[j, lines, :], rowr.at[j, lines, :]
         if d == 0:
             return pltpu.make_async_copy(s, t, rl.at[j])
-        return remote(s, t, rs.at[j, d], rr.at[j, d], pdev(npl - d))
-
-    def back(j):
+        return remote(s, t, rs.at[j], rr.at[j], pdev(npl - d))
+
+    def rall(j):
+        lines = pl.ds(cap, batch - cap)
+        return remote(
+            rows.at[j, lines, :], rowr.at[j, lines, :], rs.at[j], rr.at[j], pdev(1 % npl)
+        )
+
+    def gather(j):
         total = red[j, :, cols(c)].astype(jnp.float32)
         for d in range(1, ntp):
             dcopy(j, d).wait_recv()
-            total = total + redr[j, d].astype(jnp.float32)
+            total = total + redr[j, d - 1].astype(jnp.float32)
         rows[j] = total.astype(jnp.bfloat16)
+
+    def back(j):
+        gather(j)
         for d in range(1, npl):
             rcopy(j, d).start()
         rcopy(j, 0).start()
 
+    def ncopy(slot, to):
+        return remote(
+            rows.at[1], near.at[slot], ns.at[0], nr.at[slot], {"ep": mirror(to) * npl + p}
+        )
+
+    def hand():
+        gather(1)
+
+        @pl.when(w < half - 1)
+        def _():
+            ncopy(0, w + 1).start()
+
+        @pl.when(w == half - 1)
+        def _():
+            ncopy(1, w + 1).start()
+
+    def ecopy(d):
+        return remote(ids, seen.at[d], es.at[0], er.at[0], pdev(d))
+
+    def eall():
+        view = seen.at[pl.ds(1, npl - 1)]
+        return remote(view, view, es.at[0], er.at[0], pdev(1 % npl))
+
+    def hcopy(d):
+        return remote(home.at[d], homer.at[d], hs.at[0], hr.at[0], pdev(npl - d))
+
+    def hall():
+        some = pl.ds(1, npl - 1)
+        return remote(home.at[some], homer.at[some], hs.at[0], hr.at[0], pdev(1 % npl))
+
+    def fold(slot, holds, block):
+        @pl.when(holds)
+        def _():
+            ncopy(slot, w + 1).wait_recv()
+            for d in range(npl):
+                named = ids[...] if d == 0 else seen[d]
+                sel = choose(named, mirror(block) * npl + p)[1].astype(jnp.bfloat16)
+                acc[d] += tn(sel, near[slot, d * cap:(d + 1) * cap, :])
+
+    def homeward():
+        gather(0)
+        if npl > 1:
+            eall().wait_recv()
+        for d in range(npl):
+            named = ids[...] if d == 0 else seen[d]
+            sel = choose(named, z * npl + p)[1].astype(jnp.bfloat16)
+            acc[d] = tn(sel, rows[0, d * cap:(d + 1) * cap, :])
+        if nz > 1:
+            fold(0, inner, w - 1)
+            fold(1, w == half - 1, w + 1)
+        for d in range(npl):
+            home[d] = acc[d].astype(jnp.bfloat16)
+            if d:
+                hcopy(d).start()
+
     def qcopy(j):
         return remote(
             part.at[j], partr.at[z], qs.at[j], qr.at[z], {"ep": source(j) * npl + p}
@@ -283,8 +341,8 @@
         remote(part.at[j], partr.at[here], qs.at[j], qr.at[here], zdev(1)).wait_recv()
 
     def combine(j):
-        for d in range(1, npl):
-            rcopy(j, d).wait_recv()
+        if npl > 1:
+            rall(j).wait_recv()
         rcopy(j, 0).wait()
         part[j] = tn(oh[j], rowr[j]).astype(jnp.bfloat16)
         if j:
@@ -301,8 +359,31 @@
             out[0, :, here] = nn(left[...], right[:, here]).astype(jnp.bfloat16)
 
     last = nz - 1
-    send_x(0)
-    send_c(0)
+    for copy in inputs[:3]:
+        copy.wait()
+    pick_x(0)
+    inputs[3].wait()
+    pick_c(0)
+    pl.semaphore_wait(barrier, len(peers) + (w + nz - 1) // nz)
+    for kind in range(4):
+        if nz > 1:
+            zfirst(kind, 1).start()
+
+            @pl.when(inner)
+            def _():
+                zfirst(kind, -1).start()
+
+    weights = [
+        pltpu.make_async_copy(h.at[0], v, s_w.at[i])
+        for i, (h, v) in enumerate(((wg_hbm, wg), (wu_hbm, wu), (wd_hbm, wd)))
+    ]
+    for copy in weights:
+        copy.start()
+
+    spread(0, 0)
+    for d in range(1, npl):
+        ecopy(d).start()
+    spread(1, 0)
     forward(0, 0)
     for i in range(1, nz):
         early(0, i)
@@ -310,6 +391,8 @@
         if i == 1:
             weights[0].wait()
             weights[1].wait()
+        if i == 3:
+            hand()
         up(i - 1)
         forward(1, i - 1)
         early(1, i)
@@ -317,37 +400,53 @@
         if i == 1:
             weights[2].wait()
         if i == last:
-            for j in range(1, last - 1):
+            for j in range(2, last - 1):
                 back(j)
         down(i - 1)
         forward(0, i)
     if nz == 1:
         for copy in weights:
             copy.wait()
-    if last > 1:
+    if last == 2:
+        hand()
+    if last > 2:
         back(last - 1)
     up(last)
     forward(1, last)
     down(last)
-    if last:
+    for j in range(2, last):
+        combine(j)
+    if last > 1:
         back(last)
-    for j in range(1, last - 1):
-        combine(j)
+    if last == 1:
+        hand()
+    homeward()
     grads(0)
     if last > 1:
-        combine(last - 1)
-    back(0)
+        combine(last)
     grads(1)
-    if last:
-        combine(last)
     grads(2)
-    combine(0)
-
-    total = part[0].astype(jnp.float32)
-    for j in range(1, nz):
-        qwait(j)
-        total = total + partr[source(j)].astype(jnp.float32)
-    ig[...] = total.astype(jnp.bfloat16)
+
+    acc[0] = home[0].astype(jnp.float32)
+    if npl > 1:
+        hall().wait_recv()
+    for d in range(1, npl):
+        acc[0] += homer[d].astype(jnp.float32)
+    for j in range(2, nz):
+
+        @pl.when(w == 0 if j == 2 else w >= 0)
+        def _():
+            qwait(j)
+            acc[0] += partr[source(j)].astype(jnp.float32)
+
+    if nz > 1:
+
+        @pl.when(w < half - 1)
+        def _():
+            qwait(1)
+            acc[0] += partr[source(1)].astype(jnp.float32)
+
+    ig[...] = acc[0].astype(jnp.bfloat16)
     if nz > 1:
         for kind in range(4):
             zfirst(kind, 1).wait_send()
@@ -364,17 +463,22 @@
                     for kind in range(4):
                         zsend(kind, w + off, w + side).wait_send()
 
+    if nz > 1:
+        ncopy(0, w + 1).wait_send()
+    if npl > 1:
+        eall().wait_send()
+        hall().wait_send()
     for j in range(nz):
-        if j:
+        if j > 1:
             qcopy(j).wait_send()
-        for d in range(1, npl):
-            pcopy(0, j, d).wait_send()
-            pcopy(1, j, d).wait_send()
-            rcopy(j, d).wait_send()
+        if npl > 1:
+            pall(0, j).wait_send()
+            pall(1, j).wait_send()
+            if j > 1:
+                rall(j).wait_send()
         for d in range(1, ntp):
-            for q in range(npl):
-                tcopy(0, j, d, q, c).wait_send()
-                tcopy(1, j, d, q, c).wait_send()
+            tcopy(0, j, d, 0, npl, c).wait_send()
+            tcopy(1, j, d, 0, npl, c).wait_send()
             dcopy(j, d).wait_send()
 
 
@@ -415,16 +519,20 @@
         vm((hidden, full), bf), vm((hidden, full), bf), vm((hidden, full), bf),
         vm((hidden, count), f32), vm((hidden, count), f32),
         vm((hidden, count), bf), vm((hidden, count), bf), vm((hidden, count), bf),
-        vm((nz, batch, full), bf), vm((nz, ntp, batch, width), bf),
+        vm((nz, batch, full), bf), vm((nz, max(1, ntp - 1), batch, width), bf),
         vm((nz, batch, width), bf), vm((nz, batch, width), bf),
         vm((nz, tok_count, width), bf), vm((nz, tok_count, width), bf),
+        vm((2, batch, width), bf), vm((npl, top, tok_count), jnp.int32),
+        vm((npl, tok_count, width), bf), vm((npl, tok_count, width), bf),
+        vm((npl, tok_count, width), f32),
         dma((4,)), dma((3,)),
         dma((4, nz + 1)), dma((4, nz)),
-        dma((2, nz, npl)), dma((2, nz, npl)), dma((2, nz)),
-        dma((2, nz, npl, ntp)), dma((2, nz, npl, ntp)),
-        dma((nz, ntp)), dma((nz, ntp)),
-        dma((nz, npl)), dma((nz, npl)), dma((nz,)),
-        dma((nz,)), dma((nz,)),
+        dma((2, nz)), dma((2, nz, max(1, npl - 1))), dma((2, nz)),
+        dma((2, nz, max(1, ntp - 1))), dma((2, nz, max(1, ntp - 1))),
+        dma((nz, max(1, ntp - 1))), dma((nz, max(1, ntp - 1))),
+        dma((nz,)), dma((nz,)), dma((nz,)),
+        dma((nz,)), dma((nz,)), dma((1,)), dma((2,)),
+        dma((1,)), dma((1,)), dma((1,)), dma((1,)),
     ]
     inside = pl.BlockSpec(memory_space=pltpu.VMEM)
     outside = pl.BlockSpec(memory_space=pl.ANY)
@@ -436,7 +544,7 @@
         out_specs=(inside,) * 4,
         scratch_shapes=scratch,
         compiler_params=pltpu.CompilerParams(
-            collective_id=0, has_side_effects=True, vmem_limit_bytes=50 * 1024 * 1024
+            collective_id=0, has_side_effects=True, vmem_limit_bytes=53 * 1024 * 1024
         ),
     )(tokens, cotangent, expert_ids.T, gate_values.T, w_gate, w_up, w_down)
     return pl.pallas_call(

time: 93.3 us -> 87.5 us (0.938)
  Pallas kernels: 92.3 us -> 86.5 us
    pallas_call x1, Pallas kernels: 88.8 us -> 83 us  [local(): pl.pallas_call(functools.partial(kernel, nz, npl, ntp, cap), out_shape=tu...]
where the time goes in v2:
time: 87.5 us; the launch traced here: 87.3 us
  Pallas kernels  86.5 us (99%)
    pallas_call x1, Pallas kernels, local(): pl.pallas_call(functools.partial(kernel, nz, npl, ntp, cap), out_shape=tu...  83 us
    pallas_call x1, Pallas kernels, local(): pl.pallas_call(finish, out_shape=tuple((jax.ShapeDtypeStruct(shape, bf) f...  3.52 us

profile of v2, /device:TPU:0, one launch (start us, length us, event | category | flops | bytes accessed | tf_op | source)
XLA Modules:
  0.0 87.3 jit_solution(14618501128446190663)
XLA Ops:
  0.6 83.0 %shard_map.102 = (bf16[128,1024]{1,0:T(8,128)(2,1)S(1)}, bf16[1,704,2048]{2,1,0:T(8,128)(2,1)S(1)}, bf16[1,704,2048]{2,1,0:T(8,128)(2,1)S(1)}, bf16[1,704,2048]{2,1,0:T(8,128)(2,1)S(1)}) custom-call(bf16[128,1024]{1,0:T(8,128)(2,1)} %tok_hbm.1, bf16[128,1024]{1,0:T(8,128)(2,1)} %cot_hbm.1, s32[6,128]{1,0:T(8,128)} %bitcast.2, f32[6,128]{1,0:T(8,128)} %bitcast.3, ...), custom_call_target="tpu_custom_call" | custom-call | tf_op jit(solution)/shard_map/pallas_call | solution.py:540
  83.7 3.5 %shard_map.103 = (bf16[128,1024]{1,0:T(8,128)(2,1)}, bf16[1,704,2048]{2,1,0:T(8,128)(2,1)}, bf16[1,704,2048]{2,1,0:T(8,128)(2,1)}, bf16[1,704,2048]{2,1,0:T(8,128)(2,1)}) custom-call(bf16[128,1024]{1,0:T(8,128)(2,1)S(1)} %get-tuple-element.8.ig, bf16[1,704,2048]{2,1,0:T(8,128)(2,1)S(1)} %get-tuple-element.9.gg, ...), custom_call_target="tpu_custom_call" | custom-call | tf_op jit(solution)/shard_map/pallas_call | solution.py:550

commit v3 on v2

--- a/solution.py
+++ b/solution.py
@@ -250,17 +250,23 @@
             if d:
                 dcopy(j, d).start()
 
-    def rcopy(j, d):
+    wide = width // 2
+
+    def strip(h):
+        return pl.ds(h * wide, wide)
+
+    def rcopy(j, d, h):
         lines = pl.ds(d * cap, cap)
-        s, t = rows.at[j, lines, :], rowr.at[j, lines, :]
+        s, t = rows.at[j, lines, strip(h)], rowr.at[j, lines, strip(h)]
         if d == 0:
-            return pltpu.make_async_copy(s, t, rl.at[j])
-        return remote(s, t, rs.at[j], rr.at[j], pdev(npl - d))
-
-    def rall(j):
+            return pltpu.make_async_copy(s, t, rl.at[j, h])
+        return remote(s, t, rs.at[j, h], rr.at[j, h], pdev(npl - d))
+
+    def rall(j, h):
         lines = pl.ds(cap, batch - cap)
         return remote(
-            rows.at[j, lines, :], rowr.at[j, lines, :], rs.at[j], rr.at[j], pdev(1 % npl)
+            rows.at[j, lines, strip(h)], rowr.at[j, lines, strip(h)],
+            rs.at[j, h], rr.at[j, h], pdev(1 % npl),
         )
 
     def gather(j):
@@ -272,9 +278,10 @@
 
     def back(j):
         gather(j)
-        for d in range(1, npl):
-            rcopy(j, d).start()
-        rcopy(j, 0).start()
+        for h in range(2):
+            for d in range(1, npl):
+                rcopy(j, d, h).start()
+            rcopy(j, 0, h).start()
 
     def ncopy(slot, to):
         return remote(
@@ -328,25 +335,25 @@
             fold(1, w == half - 1, w + 1)
         for d in range(npl):
             home[d] = acc[d].astype(jnp.bfloat16)
-            if d:
-                hcopy(d).start()
-
-    def qcopy(j):
+
+    def qcopy(j, h):
         return remote(
-            part.at[j], partr.at[z], qs.at[j], qr.at[z], {"ep": source(j) * npl + p}
+            part.at[j, :, strip(h)], partr.at[z, :, strip(h)], qs.at[j, h], qr.at[z, h],
+            {"ep": source(j) * npl + p},
         )
 
     def qwait(j):
         here = source(j)
-        remote(part.at[j], partr.at[here], qs.at[j], qr.at[here], zdev(1)).wait_recv()
-
-    def combine(j):
+        for h in range(2):
+            view = partr.at[here, :, strip(h)]
+            remote(view, view, qs.at[j, h], qr.at[here, h], zdev(1)).wait_recv()
+
+    def combine(j, h):
         if npl > 1:
-            rall(j).wait_recv()
-        rcopy(j, 0).wait()
-        part[j] = tn(oh[j], rowr[j]).astype(jnp.bfloat16)
-        if j:
-            qcopy(j).start()
+            rall(j, h).wait_recv()
+        rcopy(j, 0, h).wait()
+        part[j, :, strip(h)] = tn(oh[j], rowr[j, :, strip(h)]).astype(jnp.bfloat16)
+        qcopy(j, h).start()
 
     tile = min(512, xe.shape[1])
 
@@ -415,7 +422,8 @@
     forward(1, last)
     down(last)
     for j in range(2, last):
-        combine(j)
+        combine(j, 0)
+        combine(j, 1)
     if last > 1:
         back(last)
     if last == 1:
@@ -423,7 +431,11 @@
     homeward()
     grads(0)
     if last > 1:
-        combine(last)
+        combine(last, 0)
+    for d in range(1, npl):
+        hcopy(d).start()
+    if last > 1:
+        combine(last, 1)
     grads(1)
     grads(2)
 
@@ -470,12 +482,14 @@
         hall().wait_send()
     for j in range(nz):
         if j > 1:
-            qcopy(j).wait_send()
+            qcopy(j, 0).wait_send()
+            qcopy(j, 1).wait_send()
         if npl > 1:
             pall(0, j).wait_send()
             pall(1, j).wait_send()
             if j > 1:
-                rall(j).wait_send()
+                rall(j, 0).wait_send()
+                rall(j, 1).wait_send()
         for d in range(1, ntp):
             tcopy(0, j, d, 0, npl, c).wait_send()
             tcopy(1, j, d, 0, npl, c).wait_send()
@@ -530,8 +544,8 @@
         dma((2, nz)), dma((2, nz, max(1, npl - 1))), dma((2, nz)),
         dma((2, nz, max(1, ntp - 1))), dma((2, nz, max(1, ntp - 1))),
         dma((nz, max(1, ntp - 1))), dma((nz, max(1, ntp - 1))),
-        dma((nz,)), dma((nz,)), dma((nz,)),
-        dma((nz,)), dma((nz,)), dma((1,)), dma((2,)),
+        dma((nz, 2)), dma((nz, 2)), dma((nz, 2)),
+        dma((nz, 2)), dma((nz, 2)), dma((1,)), dma((2,)),
         dma((1,)), dma((1,)), dma((1,)), dma((1,)),
     ]
     inside = pl.BlockSpec(memory_space=pltpu.VMEM)

time: 87.5 us -> 86.1 us (0.984)
  Pallas kernels: 86.5 us -> 85.1 us
    pallas_call x1, Pallas kernels: 83 us -> 81.6 us  [local(): pl.pallas_call(functools.partial(kernel, nz, npl, ntp, cap), out_shape=tu...]
where the time goes in v3:
time: 86.1 us; the launch traced here: 85.9 us
  Pallas kernels  85.1 us (99%)
    pallas_call x1, Pallas kernels, local(): pl.pallas_call(functools.partial(kernel, nz, npl, ntp, cap), out_shape=tu...  81.6 us
    pallas_call x1, Pallas kernels, local(): pl.pallas_call(finish, out_shape=tuple((jax.ShapeDtypeStruct(shape, bf) f...  3.52 us

profile of v3, /device:TPU:0, one launch (start us, length us, event | category | flops | bytes accessed | tf_op | source)
XLA Modules:
  0.0 85.9 jit_solution(5994228277356155968)
XLA Ops:
  0.6 81.6 %shard_map.102 = (bf16[128,1024]{1,0:T(8,128)(2,1)S(1)}, bf16[1,704,2048]{2,1,0:T(8,128)(2,1)S(1)}, bf16[1,704,2048]{2,1,0:T(8,128)(2,1)S(1)}, bf16[1,704,2048]{2,1,0:T(8,128)(2,1)S(1)}) custom-call(bf16[128,1024]{1,0:T(8,128)(2,1)} %tok_hbm.1, bf16[128,1024]{1,0:T(8,128)(2,1)} %cot_hbm.1, s32[6,128]{1,0:T(8,128)} %bitcast.2, f32[6,128]{1,0:T(8,128)} %bitcast.3, ...), custom_call_target="tpu_custom_call" | custom-call | tf_op jit(solution)/shard_map/pallas_call | solution.py:554
  82.3 3.5 %shard_map.103 = (bf16[128,1024]{1,0:T(8,128)(2,1)}, bf16[1,704,2048]{2,1,0:T(8,128)(2,1)}, bf16[1,704,2048]{2,1,0:T(8,128)(2,1)}, bf16[1,704,2048]{2,1,0:T(8,128)(2,1)}) custom-call(bf16[128,1024]{1,0:T(8,128)(2,1)S(1)} %get-tuple-element.8.ig, bf16[1,704,2048]{2,1,0:T(8,128)(2,1)S(1)} %get-tuple-element.9.gg, ...), custom_call_target="tpu_custom_call" | custom-call | tf_op jit(solution)/shard_map/pallas_call | solution.py:564
